TPU v7x, 512 devices: a 8x2x16 block of a 8x8x16 slice. The times are simulated.
512 devices in a mesh: grp: 2 (over y), tx: 16 (over z), ty: 16 (over x, core).
Axes of the slice: x: 8, y: 2, z: 16, core: 2. Of those that a mesh axis runs over, the one named last changes fastest.
The devices are a block of a 8x8x16 slice.
Arguments:
- obj_field: float32 [2, 4096, 2048], P(None, ('grp', 'tx'), 'ty'), parts along dimension 1, may hold values from -6 to 6
- eigenprobes: bfloat16 [2, 32, 128, 128], P(None, 'grp'), parts along dimension 1, may hold values from -1.5 to 1.5
- weights: float32 [32, 16, 3, 16], P(('grp', 'tx'), 'ty'), parts along dimension 0, may hold values from -4 to 4
- offsets: int32 [32, 16, 3, 2], P(('grp', 'tx'), 'ty'), parts along dimension 0, may hold values from 0 to 127
- counts: int32 [32, 16], P(('grp', 'tx'), 'ty'), parts along dimension 0, may hold values from 1 to 3, as said below
- amplitudes: bfloat16 [32, 16, 3, 128, 128], P(('grp', 'tx'), 'ty'), parts along dimension 0, may hold values from 0.19921875 to 3
Outputs:
- new_object: float32 [2, 4096, 2048], P(None, ('grp', 'tx'), 'ty'), parts along dimension 1
- new_eigenprobes: float32 [2, 32, 128, 128], P(None, 'grp'), parts along dimension 1
There are 2 independent parts, one for each index of `grp`. A program takes and returns all parts, laid end to end along the dimension named above; each array names one. Nothing has to cross between parts.
Inputs may be any that keep to these rules, and one draw needn't show every extreme that they name: Every tile holds 1 to 3 positions; some tile holds exactly 3; slots from counts on are unused.
All inputs are finite; a program needn't handle non-finite values.
Results may differ from a plain program's by a relative error of at most 0.0003.
Values sent between devices are 32-bit elements; how exact they have to be, the bound alone decides.
No kernel may reach another device: no remote copies, remote signals or barrier semaphores. Data moves between devices by JAX's collectives and lax.ppermute only.
A program may use at most 64 MiB of HBM per device.

v0:
```python
import functools
import math

import jax
import jax.numpy as jnp
from jax import lax
from jax.sharding import Mesh
from jax.sharding import PartitionSpec as P

TY = ("ty_0", "ty_1")
TX_TY = ("tx", "ty_0", "ty_1")


high = lax.Precision.HIGHEST


def from_behind(value, axis, steps):
    count = lax.axis_size(axis)
    pairs = [(source, (source + steps) % count) for source in range(count)]
    return lax.ppermute(value, axis, pairs)


def one_axis_at_a_time(shard, axes):
    return functools.reduce(lax.psum, axes, shard)


def in_blocks(shard, dim, count):
    before, after = (shard.shape[:dim], shard.shape[dim + 1 :])
    return jnp.moveaxis(shard.reshape(*before, count, -1, *after), dim, 0)


def sent_and_summed(shard, axis, dim):
    tiles = in_blocks(shard, dim, lax.axis_size(axis))
    arrived = lax.all_to_all(tiles, axis, split_axis=0, concat_axis=0, tiled=True)
    return arrived.sum(axis=0)


def gathered_total(shard, axis):
    return lax.all_gather(shard, axis).sum(0)


def tables(frame, sign):
    grid = jnp.arange(frame, dtype=jnp.int32)
    phase = grid[:, None] * grid[None, :] % frame
    angle = phase.astype(jnp.float32) * (2.0 * math.pi / frame)
    scale = 1.0 / math.sqrt(frame)
    return (jnp.cos(angle) * scale, sign * jnp.sin(angle) * scale)


def transform(real_part, imag_part, table_re, table_im):
    left_re = jnp.einsum("jk,skl->sjl", table_re, real_part, precision=high) - jnp.einsum(
        "jk,skl->sjl", table_im, imag_part, precision=high
    )
    left_im = jnp.einsum("jk,skl->sjl", table_re, imag_part, precision=high) + jnp.einsum(
        "jk,skl->sjl", table_im, real_part, precision=high
    )
    out_re = jnp.einsum("sjk,kl->sjl", left_re, table_re, precision=high) - jnp.einsum(
        "sjk,kl->sjl", left_im, table_im, precision=high
    )
    out_im = jnp.einsum("sjk,kl->sjl", left_re, table_im, precision=high) + jnp.einsum(
        "sjk,kl->sjl", left_im, table_re, precision=high
    )
    return (out_re, out_im)


def row_divisor(norms, start, count, frame, modes):
    mode_of_row = (start + jnp.arange(count, dtype=jnp.int32)) // frame % modes
    match = mode_of_row[:, None] == jnp.arange(modes, dtype=jnp.int32)[None, :]
    return jnp.sum(jnp.where(match, norms[None, :] + 1.0, 0.0), axis=1)


def per_device(obj_field, eigenprobes, weights, offsets, counts, amplitudes):
    tile = obj_field.shape[1]
    modes = eigenprobes.shape[1]
    frame = eigenprobes.shape[2]
    slots = weights.shape[2]
    wts = weights[0, 0]
    offs = offsets[0, 0]
    live = (jnp.arange(slots, dtype=jnp.int32) < counts[0, 0]).astype(jnp.float32)
    local_norms = jnp.sum(live[:, None] * wts * wts, axis=0)
    below = from_behind(obj_field, "tx", -1)
    tall = jnp.concatenate([obj_field, below], axis=1)
    beside = from_behind(tall, TY, -1)
    region = jnp.concatenate([tall, beside], axis=2)
    zero_index = jnp.int32(0)

    def read_window(row_start, col_start):
        return lax.dynamic_slice(region, (zero_index, row_start, col_start), (2, frame, frame))

    windows = jax.vmap(read_window)(offs[:, 0], offs[:, 1])
    win_re = windows[:, 0]
    win_im = windows[:, 1]
    eig32 = eigenprobes.astype(jnp.float32)
    probe = jnp.einsum("sk,ckij->csij", wts, eig32, precision=high)
    psi_re = probe[0] * win_re - probe[1] * win_im
    psi_im = probe[0] * win_im + probe[1] * win_re
    fwd_re, fwd_im = tables(frame, -1.0)
    spec_re, spec_im = transform(psi_re, psi_im, fwd_re, fwd_im)
    amps = amplitudes[0, 0].astype(jnp.float32)
    factor = (amps / jnp.sqrt(spec_re * spec_re + spec_im * spec_im + 0.25) - 1.0) * live[
        :, None, None
    ]
    inv_re, inv_im = tables(frame, 1.0)
    chi_re, chi_im = transform(spec_re * factor, spec_im * factor, inv_re, inv_im)
    obj_re = probe[0] * chi_re + probe[1] * chi_im
    obj_im = probe[0] * chi_im - probe[1] * chi_re
    power = (probe[0] * probe[0] + probe[1] * probe[1]) * live[:, None, None]
    pieces = jnp.stack([obj_re, obj_im, power], axis=1)

    def add_slot(slot, acc):
        row_start = offs[slot, 0]
        col_start = offs[slot, 1]
        piece = lax.dynamic_index_in_dim(pieces, slot, 0, keepdims=False)
        current = lax.dynamic_slice(acc, (zero_index, row_start, col_start), (3, frame, frame))
        return lax.dynamic_update_slice(acc, current + piece, (zero_index, row_start, col_start))

    acc = jnp.zeros((3, tile + frame, tile + frame), jnp.float32)
    acc = lax.fori_loop(0, slots, add_slot, acc)
    grad_re = win_re * chi_re + win_im * chi_im
    grad_im = win_re * chi_im - win_im * chi_re
    slot_grad = jnp.stack([grad_re, grad_im])
    spilled = from_behind(acc[:, :, tile:], TY, 1)
    merged = acc[:, :, :tile].at[:, :, :frame].add(spilled)
    dropped = from_behind(merged[:, tile:, :], "tx", 1)
    totals = merged[:, :tile, :].at[:, :frame, :].add(dropped)
    local_illum = jnp.sum(totals[2])
    norms, illum_sum = (
        one_axis_at_a_time(local_norms, TX_TY),
        one_axis_at_a_time(local_illum, TX_TY),
    )
    cells = lax.axis_size("tx") * lax.axis_size(TY) * tile * tile
    mean_illum = illum_sum / cells
    new_object = obj_field + totals[:2] / (totals[2] + mean_illum)[None]
    flat_rows = 2 * modes * frame
    flat_eig = eig32.reshape(flat_rows, frame)
    gprobe = jnp.einsum("sk,csij->ckij", wts, slot_grad, precision=high)
    flat_grad = gprobe.reshape(flat_rows, frame)
    share_rows = flat_rows // lax.axis_size("tx")
    start = lax.axis_index("tx") * share_rows
    partial_value = sent_and_summed(flat_grad, "tx", 0)
    share = gathered_total(partial_value, TY)
    own = lax.dynamic_slice_in_dim(flat_eig, start, share_rows, 0)
    updated = own + share / row_divisor(norms, start, share_rows, frame, modes)[:, None]
    new_eig = lax.all_gather(updated, "tx", axis=0, tiled=True).reshape(2, modes, frame, frame)
    return (new_object, new_eig)


def solution(mesh):
    finer = Mesh(
        mesh.devices.reshape(mesh.shape["grp"], mesh.shape["tx"], 8, 2),
        ("grp", "tx", "ty_0", "ty_1"),
    )
    return jax.shard_map(
        per_device,
        mesh=finer,
        in_specs=(
            P(None, ("grp", "tx"), TY),
            P(None, "grp", None, None),
            P(("grp", "tx"), TY, None, None),
            P(("grp", "tx"), TY, None, None),
            P(("grp", "tx"), TY),
            P(("grp", "tx"), TY, None, None, None),
        ),
        out_specs=(P(None, ("grp", "tx"), TY), P(None, "grp", None, None)),
        check_vma=False,
    )
```

profile of v0, /device:TPU:80, one launch (start us, length us, event | category | flops | bytes accessed | tf_op | source)
XLA Modules:
  0.0 367.4 jit_solution(7381467266140601053)
XLA Ops:
  7.2 44.0 %collective-permute-start = (f32[2,128,128]{2,1,0:T(8,128)}, f32[2,128,128]{2,1,0:T(8,128)S(1)}, u32[]{:S(2)}, u32[]{:S(2)}) collective-permute-start(f32[2,128,128]{2,1,0:T(8,128)} %param.16), channel_id=1, source_target_pairs={{0,240},{16,0},{32,16},{48,32},{64,48},{80,64},{96,80},{112,96},{1... | collective-permute-start | bytes 393224 | tf_op jit(solution)/shard_map/ppermute | solution.py:20
  54.4 2.5 collective-permute-start.1
  56.9 2.2 convolution_bitcast_fusion.1
  59.1 1.7 collective-permute-done.1
  60.9 15.2 %while.19 = (s32[]{:T(128)}, f32[2,256,256]{2,1,0:T(8,128)S(1)}, s32[3,3]{1,0:T(4,128)S(1)}, f32[3,2,128,128]{3,0,2,1:T(4,128)S(1)}, s32[]{:T(128)}, /*index=5*/s32[]{:T(128)}) while((s32[]{:T(128)}, f32[2,256,256]{2,1,0:T(8,128)S(1)}, s32[3,3]{1,0:T(4,128)S(1)}, f32[3,2,128,128]{3,0,2,1:T(4,128)S(1)}, s32[]{:T(128)}, /*index=5*/s32[]{:T(128)}) %tuple.75), condition=%wide.while_cond.2, body=%wide.while_body.2.sunk | while | flops 2 | bytes 524421 | solution.py:88
  62.8 3.1 dynamic-update-slice.11
  67.8 3.1 dynamic-update-slice.11
  72.8 3.1 dynamic-update-slice.11
  87.7 2.1 convolution_bitcast_fusion
  90.4 100.8 %all_to_all.5 = f32[16,256,128]{2,1,0:T(8,128)S(1)} all-to-all(f32[16,256,128]{2,1,0:T(8,128)S(1)} %bitcast.175), channel_id=1, replica_groups=mesh['grp'=2,'tx'=16,'ty_0'=8,'ty_1'=2] {'tx'}, dimensions={0} | all-to-all | bytes 4194304 | tf_op jit(solution)/shard_map/all_to_all | solution.py:34
  192.6 21.0 %while.18 = (s32[]{:T(128)}, f32[3,256,256]{2,1,0:T(8,128)S(1)}, s32[3,2]{0,1:T(2,128)S(1)}, f32[3,3,128,128]{3,0,2,1:T(4,128)S(1)}, s32[]{:T(128)}, /*index=5*/s32[]{:T(128)}, s32[]{:T(128)}) while((s32[]{:T(128)}, f32[3,256,256]{2,1,0:T(8,128)S(1)}, s32[3,2]{0,1:T(2,128)S(1)}, f32[3,3,128,128]{3,0,2,1:T(4,128)S(1)}, s32[]{:T(128)}, ...), condition=%wide.region_1.2_spmd, body=%wide.region_0.0_spmd.sunk | while | flops 49160 | bytes 1376445 | solution.py:118
  197.3 1.5 dynamic_update_slice.8
  203.4 2.9 dynamic_update_slice.8
  210.9 2.7 dynamic_update_slice.8
  213.8 13.1 %collective-permute-done.2 = f32[3,256,128]{2,1,0:T(8,128)S(1)} collective-permute-done((f32[3,256,128]{2,1,0:T(8,128)S(1)}, f32[3,256,128]{2,1,0:T(8,128)S(1)}, u32[]{:S(2)}, u32[]{:S(2)}) %collective-permute-start.2) | collective-permute-done | bytes 393248 | tf_op jit(solution)/shard_map/ppermute | solution.py:20
  227.0 3.4 collective-permute-start.3
  230.5 7.0 %collective-permute-done.3 = f32[3,128,128]{2,1,0:T(8,128)S(1)} collective-permute-done((f32[3,128,128]{2,1,0:T(8,128)S(1)}, f32[3,128,128]{2,1,0:T(8,128)S(1)}, u32[]{:S(2)}, u32[]{:S(2)}) %collective-permute-start.3) | collective-permute-done | bytes 196640 | tf_op jit(solution)/shard_map/ppermute | solution.py:20
  238.1 29.7 %all-reduce = (f32[]{:T(128)}, f32[16]{0:T(128)S(1)}) all-reduce(f32[]{:T(128)} %slice_reduce_fusion, f32[16]{0:T(128)S(1)} %fusion.80), channel_id=1, replica_groups=mesh['grp'=2,'tx'=16,'ty_0'=8,'ty_1'=2] {'tx'}, use_global_device_ids=true, to_apply=%region_3.4 | all-reduce | flops 17 | bytes 136 | tf_op jit(solution)/shard_map/psum | solution.py:24
  267.7 15.6 %all-reduce.1 = (f32[]{:T(128)}, f32[16]{0:T(128)S(1)}) all-reduce(f32[]{:T(128)} %get-tuple-element.170, f32[16]{0:T(128)S(1)} %get-tuple-element.171), channel_id=1, replica_groups=mesh['grp'=2,'tx'=16,'ty_0'=8,'ty_1'=2] {'ty_0'}, use_global_device_ids=true, to_apply=%region_4.5 | all-reduce | flops 17 | bytes 136 | tf_op jit(solution)/shard_map/psum | solution.py:24
  283.3 3.1 all-reduce.2
  286.5 1.7 reduce_sum.47
  288.2 1.6 convert_add_fusion
  291.2 66.2 %all-gather.4.cloned.1.call-done = f32[4096,128]{1,0:T(8,128)} async-done(((f32[256,128]{1,0:T(8,128)}), f32[4096,128]{1,0:T(8,128)}) %all-gather.4.cloned.1.call-update) | async-done | bytes 2097168 | tf_op jit(solution)/shard_map/all_gather | solution.py:144
  357.4 3.1 copy.171
  (78 shorter events, 26.3 us)
Async XLA Ops:
  7.2 279.3 %all-gather.6.cloned.1.call-start = ((), (), s32[]{:S(2)}) async-start(), calls=%async_computation.2 | async-start | bytes 2228224 | tf_op jit(solution)/shard_map/all_gather | solution.py:39
  7.2 47.1 %collective-permute-start = (f32[2,128,128]{2,1,0:T(8,128)}, f32[2,128,128]{2,1,0:T(8,128)S(1)}, u32[]{:S(2)}, u32[]{:S(2)}) collective-permute-start(f32[2,128,128]{2,1,0:T(8,128)} %param.16), channel_id=1, source_target_pairs={{0,240},{16,0},{32,16},{48,32},{64,48},{80,64},{96,80},{112,96},{1... | collective-permute-start | bytes 393224 | tf_op jit(solution)/shard_map/ppermute | solution.py:20
  54.4 6.4 %collective-permute-start.1 = (f32[2,256,128]{2,1,0:T(8,128)S(1)}, f32[2,256,128]{2,1,0:T(8,128)S(1)}, u32[]{:S(2)}, u32[]{:S(2)}) collective-permute-start(f32[2,256,128]{2,1,0:T(8,128)S(1)} %constant_dynamic-update-slice_fusion), channel_id=1, source_target_pairs={{0,15},{1,0},{2,1},{3,2},{4,3},{5,4},{6,5},{7,6},{8,7},{9,8},{10,9... | collective-permute-start | bytes 786440 | tf_op jit(solution)/shard_map/ppermute | solution.py:20
  76.9 4.5 %copy-start.1 = (bf16[1,1,3,128,128]{4,3,2,1,0:T(8,128)(2,1)S(1)}, bf16[1,1,3,128,128]{4,3,2,1,0:T(8,128)(2,1)}, u32[]{:S(2)}) copy-start(bf16[1,1,3,128,128]{4,3,2,1,0:T(8,128)(2,1)} %param.21) | copy-start | bytes 294916
  85.0 2.7 copy-start.3
  191.9 0.7 copy-start.2
  192.0 165.4 %all-gather.4.cloned.1.call-start = ((), (), s32[]{:S(2)}) async-start(), calls=%async_computation.1 | async-start | bytes 2228224 | tf_op jit(solution)/shard_map/all_gather | solution.py:144
  213.7 13.2 %collective-permute-start.2 = (f32[3,256,128]{2,1,0:T(8,128)S(1)}, f32[3,256,128]{2,1,0:T(8,128)S(1)}, u32[]{:S(2)}, u32[]{:S(2)}) collective-permute-start(f32[3,256,128]{2,1,0:T(8,128)S(1)} %slice.92), channel_id=1, source_target_pairs={{0,1},{1,2},{2,3},{3,4},{4,5},{5,6},{6,7},{7,8},{8,9},{9,10},{10,1... | collective-permute-start | bytes 1179656 | tf_op jit(solution)/shard_map/ppermute | solution.py:20
  227.0 63.6 %copy-start = (f32[2,128,128]{2,1,0:T(8,128)S(1)}, f32[2,128,128]{2,1,0:T(8,128)}, u32[]{:S(2)}) copy-start(f32[2,128,128]{2,1,0:T(8,128)} %param.16) | copy-start | bytes 393220
  227.0 10.4 %collective-permute-start.3 = (f32[3,128,128]{2,1,0:T(8,128)S(1)}, f32[3,128,128]{2,1,0:T(8,128)S(1)}, u32[]{:S(2)}, u32[]{:S(2)}) collective-permute-start(f32[3,128,128]{2,1,0:T(8,128)S(1)} %slice.115), channel_id=1, source_target_pairs={{0,16},{16,32},{32,48},{48,64},{64,80},{80,96},{96,112},{112,128},... | collective-permute-start | bytes 589832 | tf_op jit(solution)/shard_map/ppermute | solution.py:20
Sparse Core Ops, SparseCore 0:
  192.1 40.3 all-gather.5
  290.0 67.3 all-gather.3
where the time goes:
time: 369 us; the launch traced here: 367 us
  blocking collectives  149 us (40%)
  waiting for transfers between devices  88.8 us (24%)
  starting transfers between devices  50.1 us (14%)
  local copies, waits for them, and re-layouts  29.7 us (8%)
  between operations  15.7 us (4%)
  matrix products  14.7 us (4%)
  loops' own time  11.4 us (3%)
  other arithmetic  7.88 us (2%)
    all_to_all x1, blocking collectives, sent_and_summed(): lax.all_to_all(tiles, axis, split_axis=0, concat_axis=0, tiled=True)  101 us
    all_gather x1, waiting for transfers between devices, per_device(): lax.all_gather(updated, 'tx', axis=0, tiled=True)  66.2 us
    ppermute x4, starting transfers between devices, from_behind(): return lax.ppermute(value, axis, pairs)  50 us
    psum x3, blocking collectives, one_axis_at_a_time(): return functools.reduce(lax.psum, axes, shard)  48.4 us
    ppermute x4, waiting for transfers between devices, from_behind(): return lax.ppermute(value, axis, pairs)  22.4 us
    gather x12, local copies, waits for them, and re-layouts  14.9 us
    another operation x1, loops' own time, per_device(): acc = lax.fori_loop(0, slots, add_slot, acc)  11.1 us
  transfers between devices with their start and end apart: 6, of which 5 were waited for; matrix products, arithmetic and copies ran while one was open for 4% of the time, Pallas kernels for 0%

commit v1 on v0

v1 whole, which is shorter than its diff:
```python
import math

import jax
import jax.numpy as jnp
from jax import lax
from jax.sharding import Mesh
from jax.sharding import PartitionSpec as P

TY = ("ty_0", "ty_1")
PART = ("tx", "ty_0", "ty_1")

high = lax.Precision.HIGHEST


def moved(value, down, right):
    rows = lax.axis_size("tx")
    cols = lax.axis_size("ty_0") * lax.axis_size("ty_1")
    pairs = [
        (i * cols + j, ((i + down) % rows) * cols + (j + right) % cols)
        for i in range(rows)
        for j in range(cols)
    ]
    return lax.ppermute(value, PART, pairs)


def exchanged(blocks, axis):
    return lax.all_to_all(blocks, axis, split_axis=0, concat_axis=0, tiled=True)


def copied_to_all(block, axis):
    count = lax.axis_size(axis)
    return exchanged(jnp.broadcast_to(block[None], (count, *block.shape)), axis)


def tables(frame, sign):
    grid = jnp.arange(frame, dtype=jnp.int32)
    phase = grid[:, None] * grid[None, :] % frame
    angle = phase.astype(jnp.float32) * (2.0 * math.pi / frame)
    scale = 1.0 / math.sqrt(frame)
    return (jnp.cos(angle) * scale, sign * jnp.sin(angle) * scale)


def transform(real_part, imag_part, table_re, table_im):
    left_re = jnp.einsum("jk,skl->sjl", table_re, real_part, precision=high) - jnp.einsum(
        "jk,skl->sjl", table_im, imag_part, precision=high
    )
    left_im = jnp.einsum("jk,skl->sjl", table_re, imag_part, precision=high) + jnp.einsum(
        "jk,skl->sjl", table_im, real_part, precision=high
    )
    out_re = jnp.einsum("sjk,kl->sjl", left_re, table_re, precision=high) - jnp.einsum(
        "sjk,kl->sjl", left_im, table_im, precision=high
    )
    out_im = jnp.einsum("sjk,kl->sjl", left_re, table_im, precision=high) + jnp.einsum(
        "sjk,kl->sjl", left_im, table_re, precision=high
    )
    return (out_re, out_im)


def per_device(obj_field, eigenprobes, weights, offsets, counts, amplitudes):
    tile = obj_field.shape[1]
    modes = eigenprobes.shape[1]
    frame = eigenprobes.shape[2]
    slots = weights.shape[2]
    n_tx = lax.axis_size("tx")
    n_chip = lax.axis_size("ty_0")
    n_core = lax.axis_size("ty_1")
    n_ty = n_chip * n_core
    share = frame // n_chip
    per_tx = modes // n_tx
    wts = weights[0, 0]
    offs = offsets[0, 0]
    live = (jnp.arange(slots, dtype=jnp.int32) < counts[0, 0]).astype(jnp.float32)
    live_wts = live[:, None] * wts
    below = moved(obj_field, -1, 0)
    beside = moved(obj_field, 0, -1)
    corner = moved(obj_field, -1, -1)
    region = jnp.concatenate(
        [
            jnp.concatenate([obj_field, beside], axis=2),
            jnp.concatenate([below, corner], axis=2),
        ],
        axis=1,
    )
    zero_index = jnp.int32(0)
    windows = jnp.stack(
        [
            lax.dynamic_slice(region, (zero_index, offs[s, 0], offs[s, 1]), (2, frame, frame))
            for s in range(slots)
        ]
    )
    win_re = windows[:, 0]
    win_im = windows[:, 1]
    eig32 = eigenprobes.astype(jnp.float32)
    probe = jnp.einsum("sk,ckij->csij", wts, eig32, precision=high)
    psi_re = probe[0] * win_re - probe[1] * win_im
    psi_im = probe[0] * win_im + probe[1] * win_re
    fwd_re, fwd_im = tables(frame, -1.0)
    spec_re, spec_im = transform(psi_re, psi_im, fwd_re, fwd_im)
    amps = amplitudes[0, 0].astype(jnp.float32)
    factor = (amps / jnp.sqrt(spec_re * spec_re + spec_im * spec_im + 0.25) - 1.0) * live[
        :, None, None
    ]
    inv_re, inv_im = tables(frame, 1.0)
    chi_re, chi_im = transform(spec_re * factor, spec_im * factor, inv_re, inv_im)
    grad_re = win_re * chi_re + win_im * chi_im
    grad_im = win_re * chi_im - win_im * chi_re
    power = (probe[0] * probe[0] + probe[1] * probe[1]) * live[:, None, None]
    local_illum = jnp.sum(power)

    grads = jnp.stack([grad_re, grad_im]).reshape(2, slots, n_chip, share, frame)
    grads = grads.transpose(2, 0, 1, 3, 4).reshape(n_ty, slots * share, frame)
    note = jnp.zeros((8, frame), jnp.float32)
    note = note.at[0, : slots * modes].set(live_wts.reshape(-1))
    note = note.at[1, :].set(local_illum)
    packed = jnp.concatenate([grads, jnp.broadcast_to(note[None], (n_ty, 8, frame))], axis=1)
    row = exchanged(packed, TY)
    row_wts = row[:, slots * share, : slots * modes].reshape(n_ty * slots, modes)
    row_grads = row[:, : slots * share].reshape(n_ty * slots, share, frame)
    row_illum = jnp.sum(row[:, slots * share + 1, 0])
    mode_grads = jnp.einsum("pk,pij->kij", row_wts, row_grads, precision=high)
    row_norms = jnp.sum(row_wts * row_wts, axis=0)
    tail = jnp.broadcast_to(row_norms[:, None, None], (modes, 4, frame))
    tail = jnp.concatenate([tail, jnp.full((modes, 4, frame), row_illum)], axis=1)
    sent = jnp.concatenate([mode_grads, tail], axis=1)
    total = exchanged(sent, "tx").reshape(n_tx, per_tx, share + 8, frame).sum(axis=0)
    illum_sum = total[0, share + 4, 0]
    start_mode = lax.axis_index("tx") * per_tx
    core = lax.axis_index("ty_1")
    own = lax.dynamic_slice(
        eigenprobes,
        (core, start_mode, lax.axis_index("ty_0") * share, zero_index),
        (1, per_tx, share, frame),
    )[0].astype(jnp.float32)
    updated = own + total[:, :share] / (total[:, share : share + 1] + 1.0)
    column = copied_to_all(updated, "tx").reshape(modes, share, frame)
    half = copied_to_all(column, "ty_0").reshape(n_chip, modes, share, frame)
    other = lax.ppermute(half, "ty_1", [(0, 1), (1, 0)])
    half = half.transpose(1, 0, 2, 3).reshape(modes, frame, frame)
    other = other.transpose(1, 0, 2, 3).reshape(modes, frame, frame)
    first = core == 0
    new_eig = jnp.stack([jnp.where(first, half, other), jnp.where(first, other, half)])

    obj_re = probe[0] * chi_re + probe[1] * chi_im
    obj_im = probe[0] * chi_im - probe[1] * chi_re
    pieces = jnp.stack([obj_re, obj_im, power], axis=1)
    acc = jnp.zeros((3, tile + frame, tile + frame), jnp.float32)
    for s in range(slots):
        at = (zero_index, offs[s, 0], offs[s, 1])
        current = lax.dynamic_slice(acc, at, (3, frame, frame))
        acc = lax.dynamic_update_slice(acc, current + pieces[s], at)
    from_left = moved(acc[:, :tile, tile:], 0, 1)
    from_above = moved(acc[:, tile:, :tile], 1, 0)
    from_corner = moved(acc[:, tile:, tile:], 1, 1)
    totals = acc[:, :tile, :tile] + from_left + from_above + from_corner
    cells = n_tx * n_ty * tile * tile
    mean_illum = illum_sum / cells
    new_object = obj_field + totals[:2] / (totals[2] + mean_illum)[None]
    return (new_object, new_eig)


def solution(mesh):
    finer = Mesh(
        mesh.devices.reshape(mesh.shape["grp"], mesh.shape["tx"], -1, 2),
        ("grp", "tx", "ty_0", "ty_1"),
    )
    return jax.shard_map(
        per_device,
        mesh=finer,
        in_specs=(
            P(None, ("grp", "tx"), TY),
            P(None, "grp", None, None),
            P(("grp", "tx"), TY, None, None),
            P(("grp", "tx"), TY, None, None),
            P(("grp", "tx"), TY),
            P(("grp", "tx"), TY, None, None, None),
        ),
        out_specs=(P(None, ("grp", "tx"), TY), P(None, "grp", None, None)),
        check_vma=False,
    )
```

time: 369 us -> 199 us (0.54)
  blocking collectives: 149 us -> 41.3 us
  waiting for transfers between devices: 88.8 us -> 39.6 us
  starting transfers between devices: 50.1 us -> 66.5 us
  local copies, waits for them, and re-layouts: 29.7 us -> 16.3 us
  loops' own time: 11.4 us -> 0 us
    all_gather x2 -> x0, waiting for transfers between devices: 66.2 us -> none  [the longest x1 66.2 us: per_device(): lax.all_gather(updated, 'tx', axis=0, tiled=True)]
    all_to_all x1 -> x2, blocking collectives: 101 us -> 41.3 us  [exchanged(): return lax.all_to_all(blocks, axis, split_axis=0, concat_axis=0, tiled=True)]
    psum x3 -> x0, blocking collectives: 48.4 us -> none  [one_axis_at_a_time(): return functools.reduce(lax.psum, axes, shard)]
    all_to_all x0 -> x2, waiting for transfers between devices: none -> 31.4 us  [exchanged(): return lax.all_to_all(blocks, axis, split_axis=0, concat_axis=0, tiled=True)]
    gather x12 -> x0, local copies, waits for them, and re-layouts: 14.9 us -> none
    ppermute x4 -> x7, waiting for transfers between devices: 22.4 us -> 8.2 us  [the longest x6 8.2 us: moved(): return lax.ppermute(value, PART, pairs)]
    another operation x2 -> x0, loops' own time: 11.4 us -> none  [the longest x1 11.1 us: per_device(): acc = lax.fori_loop(0, slots, add_slot, acc)]
    ppermute x4 -> x7, starting transfers between devices: 50 us -> 58.8 us  [the longest x6 56.9 us: moved(): return lax.ppermute(value, PART, pairs)]
  transfers between devices with their start and end apart: 6 -> 9, of which waited for: 5 -> 4; matrix products, arithmetic and copies ran while one was open for 4% -> 8% of each run, Pallas kernels for 0% -> 0%
where the time goes in v1:
time: 199 us; the launch traced here: 198 us
  starting transfers between devices  66.5 us (33%)
  blocking collectives  41.3 us (21%)
  waiting for transfers between devices  39.6 us (20%)
  local copies, waits for them, and re-layouts  16.3 us (8%)
  matrix products  14.2 us (7%)
  between operations  13.5 us (7%)
  other arithmetic  6.26 us (3%)
    ppermute x6, starting transfers between devices, moved(): return lax.ppermute(value, PART, pairs)  56.9 us
    all_to_all x2, blocking collectives, exchanged(): return lax.all_to_all(blocks, axis, split_axis=0, concat_axis=0, tiled=True)  41.3 us
    all_to_all x2, waiting for transfers between devices, exchanged(): return lax.all_to_all(blocks, axis, split_axis=0, concat_axis=0, tiled=True)  31.4 us
    dynamic_update_slice x3, local copies, waits for them, and re-layouts, per_device(): acc = lax.dynamic_update_slice(acc, current + pieces[s], at)  8.48 us
    ppermute x6, waiting for transfers between devices, moved(): return lax.ppermute(value, PART, pairs)  8.2 us
    all_to_all x2, starting transfers between devices, exchanged(): return lax.all_to_all(blocks, axis, split_axis=0, concat_axis=0, tiled=True)  7.73 us
  transfers between devices with their start and end apart: 9, of which 4 were waited for; matrix products, arithmetic and copies ran while one was open for 8% of the time, Pallas kernels for 0%

profile of v1, /device:TPU:80, one launch (start us, length us, event | category | flops | bytes accessed | tf_op | source)
XLA Modules:
  0.0 197.7 jit_solution(3120776916202753775)
XLA Ops:
  0.6 44.2 %collective-permute-start.1 = (f32[2,128,128]{2,1,0:T(8,128)}, f32[2,128,128]{2,1,0:T(8,128)S(1)}, u32[]{:S(2)}, u32[]{:S(2)}) collective-permute-start(f32[2,128,128]{2,1,0:T(8,128)} %param.10), channel_id=1, source_target_pairs={{0,240},{1,241},{2,242},{3,243},{4,244},{5,245},{6,246},{7,247},{8... | collective-permute-start | bytes 393224 | tf_op jit(solution)/shard_map/ppermute | solution.py:23
  44.8 3.1 %collective-permute-start = (f32[2,128,128]{2,1,0:T(8,128)}, f32[2,128,128]{2,1,0:T(8,128)S(1)}, u32[]{:S(2)}, u32[]{:S(2)}) collective-permute-start(f32[2,128,128]{2,1,0:T(8,128)} %param.10), channel_id=1, source_target_pairs={{0,15},{1,0},{2,1},{3,2},{4,3},{5,4},{6,5},{7,6},{8,7},{9,8},{10,9... | collective-permute-start | bytes 393224 | tf_op jit(solution)/shard_map/ppermute | solution.py:23
  47.9 2.3 %collective-permute-start.2 = (f32[2,128,128]{2,1,0:T(8,128)}, f32[2,128,128]{2,1,0:T(8,128)S(1)}, u32[]{:S(2)}, u32[]{:S(2)}) collective-permute-start(f32[2,128,128]{2,1,0:T(8,128)} %param.10), channel_id=1, source_target_pairs={{0,255},{1,240},{2,241},{3,242},{4,243},{5,244},{6,245},{7,246},{8... | collective-permute-start | bytes 393224 | tf_op jit(solution)/shard_map/ppermute | solution.py:23
  50.2 2.2 %fusion.4 = f32[2,128,128,3]{2,3,1,0:T(4,128)S(1)} fusion(bf16[2,16,128,128]{3,2,1,0:T(8,128)(2,1)} %param.11, f32[1,1,3,16]{3,1,2,0:T(1,128)} %param.12), kind=kOutput, calls=%fused_computation.13 | convolution fusion | flops 18874368 | bytes 1441984 | tf_op jit(solution)/shard_map/sk,ckij->csij/dot_general | solution.py:94
  52.4 1.6 fusion.173
  77.3 1.4 multiply_add_fusion
  79.6 18.7 %all_to_all.20 = f32[16,56,128]{2,1,0:T(8,128)S(1)} all-to-all(f32[16,56,128]{2,1,0:T(8,128)S(1)} %pad_maximum_fusion.2), channel_id=1, replica_groups=mesh['grp'=2,'tx'=16,'ty_0'=8,'ty_1'=2] {'ty_0','ty_1'}, dimensions={0} | all-to-all | bytes 917504 | tf_op jit(solution)/shard_map/all_to_all | solution.py:27
  101.2 4.0 %all-to-all-start.1 = ((f32[16,24,128]{2,1,0:T(8,128)}), f32[16,24,128]{2,1,0:T(8,128)S(1)}, u32[]{:S(2)}, u32[]{:S(2)}) async-start(f32[16,24,128]{2,1,0:T(8,128)} %copy.161), calls=%async_computation.1 | async-start | bytes 393216 | tf_op jit(solution)/shard_map/all_to_all | solution.py:27
  105.2 14.2 %all-to-all-done.1 = f32[16,24,128]{2,1,0:T(8,128)S(1)} async-done(((f32[16,24,128]{2,1,0:T(8,128)}), f32[16,24,128]{2,1,0:T(8,128)S(1)}, u32[]{:S(2)}, u32[]{:S(2)}) %all-to-all-start.1) | async-done | bytes 196640 | tf_op jit(solution)/shard_map/all_to_all | solution.py:27
  120.1 22.5 %all_to_all.21 = f32[16,1,16,128]{3,2,1,0:T(8,128)S(1)} all-to-all(f32[16,1,16,128]{3,2,1,0:T(8,128)S(1)} %broadcast_in_dim.24), channel_id=1, replica_groups=mesh['grp'=2,'tx'=16,'ty_0'=8,'ty_1'=2] {'tx'}, dimensions={0} | all-to-all | bytes 262144 | tf_op jit(solution)/shard_map/all_to_all | solution.py:27
  142.6 1.1 broadcast_in_dim.26
  143.7 3.8 %all-to-all-start.3 = ((f32[8,16,16,128]{3,2,1,0:T(8,128)}), f32[8,16,16,128]{3,2,1,0:T(8,128)S(1)}, u32[]{:S(2)}, u32[]{:S(2)}) async-start(f32[8,16,16,128]{3,2,1,0:T(8,128)} %broadcast_in_dim.26), calls=%async_computation.3 | async-start | bytes 2097152 | tf_op jit(solution)/shard_map/all_to_all | solution.py:27
  147.7 2.7 %dynamic_update_slice.9 = f32[3,256,256]{2,1,0:T(8,128)S(1)} dynamic-update-slice(f32[3,256,256]{2,1,0:T(8,128)S(1)} %broadcast_in_dim.18, f32[3,128,128]{2,1,0:T(8,128)S(1)} %slice_bitcast_fusion.2, s32[]{:T(128)} %constant.97.clone.1, s32[]{:T(128)S(6)} %select_n.114, s32[]{:T(128)S(6)} %select_n.115) | dynamic-update-slice | bytes 393220 | tf_op jit(solution)/shard_map/dynamic_update_slice | solution.py:150
  150.6 2.9 %dynamic_update_slice.10 = f32[3,256,256]{2,1,0:T(8,128)S(1)} dynamic-update-slice(f32[3,256,256]{2,1,0:T(8,128)S(1)} %dynamic_update_slice.9, f32[3,128,128]{2,1,0:T(8,128)S(1)} %fusion.11, s32[]{:T(128)} %constant.97.clone.1, s32[]{:T(128)S(6)} %select_n.116, s32[]{:T(128)S(6)} %select_n.117) | dynamic-update-slice | bytes 393220 | tf_op jit(solution)/shard_map/dynamic_update_slice | solution.py:150
  153.6 2.9 %dynamic_update_slice.11 = f32[3,256,256]{2,1,0:T(8,128)S(1)} dynamic-update-slice(f32[3,256,256]{2,1,0:T(8,128)S(1)} %dynamic_update_slice.10, f32[3,128,128]{2,1,0:T(8,128)S(1)} %fusion.10, s32[]{:T(128)} %constant.97.clone.1, s32[]{:T(128)S(6)} %select_n.118, s32[]{:T(128)S(6)} %select_n.119) | dynamic-update-slice | bytes 393220 | tf_op jit(solution)/shard_map/dynamic_update_slice | solution.py:150
  156.5 17.2 %all-to-all-done.3 = f32[8,16,16,128]{3,2,1,0:T(8,128)S(1)} async-done(((f32[8,16,16,128]{3,2,1,0:T(8,128)}), f32[8,16,16,128]{3,2,1,0:T(8,128)S(1)}, u32[]{:S(2)}, u32[]{:S(2)}) %all-to-all-start.3) | async-done | bytes 1048608 | tf_op jit(solution)/shard_map/all_to_all | solution.py:27
  173.7 1.1 copy.163
  174.7 1.9 collective-permute-start.6
  177.9 4.7 %collective-permute-start.5 = (f32[3,128,128]{2,1,0:T(8,128)S(1)}, f32[3,128,128]{2,1,0:T(8,128)}, u32[]{:S(2)}, u32[]{:S(2)}) collective-permute-start(f32[3,128,128]{2,1,0:T(8,128)S(1)} %get-tuple-element.31), channel_id=1, source_target_pairs={{0,17},{1,18},{2,19},{3,20},{4,21},{5,22},{6,23},{7,24},{8,25},{9,... | collective-permute-start | bytes 589832 | tf_op jit(solution)/shard_map/ppermute | solution.py:23
  182.6 2.2 %collective-permute-start.4 = (f32[3,128,128]{2,1,0:T(8,128)S(1)}, f32[3,128,128]{2,1,0:T(8,128)}, u32[]{:S(2)}, u32[]{:S(2)}) collective-permute-start(f32[3,128,128]{2,1,0:T(8,128)S(1)} %get-tuple-element.32), channel_id=1, source_target_pairs={{0,16},{1,17},{2,18},{3,19},{4,20},{5,21},{6,22},{7,23},{8,24},{9,... | collective-permute-start | bytes 589832 | tf_op jit(solution)/shard_map/ppermute | solution.py:23
  184.8 5.3 %collective-permute-done.5 = f32[3,128,128]{2,1,0:T(8,128)} collective-permute-done((f32[3,128,128]{2,1,0:T(8,128)S(1)}, f32[3,128,128]{2,1,0:T(8,128)}, u32[]{:S(2)}, u32[]{:S(2)}) %collective-permute-start.5) | collective-permute-done | bytes 196640 | tf_op jit(solution)/shard_map/ppermute | solution.py:23
  190.1 2.9 %collective-permute-done.4 = f32[3,128,128]{2,1,0:T(8,128)} collective-permute-done((f32[3,128,128]{2,1,0:T(8,128)S(1)}, f32[3,128,128]{2,1,0:T(8,128)}, u32[]{:S(2)}, u32[]{:S(2)}) %collective-permute-start.4) | collective-permute-done | bytes 196640 | tf_op jit(solution)/shard_map/ppermute | solution.py:23
  193.0 1.2 fusion.9
  196.2 1.5 pad_maximum_fusion
  (69 shorter events, 18.9 us)
Async XLA Ops:
  0.6 66.1 %copy-start = (f32[2,128,128]{2,1,0:T(8,128)S(1)}, f32[2,128,128]{2,1,0:T(8,128)}, u32[]{:S(2)}) copy-start(f32[2,128,128]{2,1,0:T(8,128)} %param.10) | copy-start | bytes 393220
  0.6 66.1 %collective-permute-start.1 = (f32[2,128,128]{2,1,0:T(8,128)}, f32[2,128,128]{2,1,0:T(8,128)S(1)}, u32[]{:S(2)}, u32[]{:S(2)}) collective-permute-start(f32[2,128,128]{2,1,0:T(8,128)} %param.10), channel_id=1, source_target_pairs={{0,240},{1,241},{2,242},{3,243},{4,244},{5,245},{6,246},{7,247},{8... | collective-permute-start | bytes 393224 | tf_op jit(solution)/shard_map/ppermute | solution.py:23
  44.8 21.9 %collective-permute-start = (f32[2,128,128]{2,1,0:T(8,128)}, f32[2,128,128]{2,1,0:T(8,128)S(1)}, u32[]{:S(2)}, u32[]{:S(2)}) collective-permute-start(f32[2,128,128]{2,1,0:T(8,128)} %param.10), channel_id=1, source_target_pairs={{0,15},{1,0},{2,1},{3,2},{4,3},{5,4},{6,5},{7,6},{8,7},{9,8},{10,9... | collective-permute-start | bytes 393224 | tf_op jit(solution)/shard_map/ppermute | solution.py:23
  47.9 18.8 %collective-permute-start.2 = (f32[2,128,128]{2,1,0:T(8,128)}, f32[2,128,128]{2,1,0:T(8,128)S(1)}, u32[]{:S(2)}, u32[]{:S(2)}) collective-permute-start(f32[2,128,128]{2,1,0:T(8,128)} %param.10), channel_id=1, source_target_pairs={{0,255},{1,240},{2,241},{3,242},{4,243},{5,244},{6,245},{7,246},{8... | collective-permute-start | bytes 393224 | tf_op jit(solution)/shard_map/ppermute | solution.py:23
  67.1 5.3 %copy-start.1 = (bf16[1,1,3,128,128]{4,3,2,1,0:T(8,128)(2,1)S(1)}, bf16[1,1,3,128,128]{4,3,2,1,0:T(8,128)(2,1)}, u32[]{:S(2)}) copy-start(bf16[1,1,3,128,128]{4,3,2,1,0:T(8,128)(2,1)} %param.15) | copy-start | bytes 294916
  101.2 18.1 %all-to-all-start.1 = ((f32[16,24,128]{2,1,0:T(8,128)}), f32[16,24,128]{2,1,0:T(8,128)S(1)}, u32[]{:S(2)}, u32[]{:S(2)}) async-start(f32[16,24,128]{2,1,0:T(8,128)} %copy.161), calls=%async_computation.1 | async-start | bytes 393216 | tf_op jit(solution)/shard_map/all_to_all | solution.py:27
  143.7 30.0 %all-to-all-start.3 = ((f32[8,16,16,128]{3,2,1,0:T(8,128)}), f32[8,16,16,128]{3,2,1,0:T(8,128)S(1)}, u32[]{:S(2)}, u32[]{:S(2)}) async-start(f32[8,16,16,128]{3,2,1,0:T(8,128)} %broadcast_in_dim.26), calls=%async_computation.3 | async-start | bytes 2097152 | tf_op jit(solution)/shard_map/all_to_all | solution.py:27
  174.7 21.3 %collective-permute-start.6 = (f32[8,16,16,128]{3,2,0,1:T(8,128)}, f32[8,16,16,128]{3,2,0,1:T(8,128)S(1)}, u32[]{:S(2)}, u32[]{:S(2)}) collective-permute-start(f32[8,16,16,128]{3,2,0,1:T(8,128)} %copy.163), channel_id=1, source_target_pairs={{0,1},{1,0},{2,3},{3,2},{4,5},{5,4},{6,7},{7,6},{8,9},{9,8},{10,11... | collective-permute-start | bytes 3145736 | tf_op jit(solution)/shard_map/ppermute | solution.py:137
  177.4 7.4 %collective-permute-start.3 = (f32[3,128,128]{2,1,0:T(8,128)}, f32[3,128,128]{2,1,0:T(8,128)}, u32[]{:S(2)}, u32[]{:S(2)}) collective-permute-start(f32[3,128,128]{2,1,0:T(8,128)} %get-tuple-element.30), channel_id=1, source_target_pairs={{0,1},{1,2},{2,3},{3,4},{4,5},{5,6},{6,7},{7,8},{8,9},{9,10},{10,1... | collective-permute-start | bytes 589832 | tf_op jit(solution)/shard_map/ppermute | solution.py:23
  177.9 12.2 %collective-permute-start.5 = (f32[3,128,128]{2,1,0:T(8,128)S(1)}, f32[3,128,128]{2,1,0:T(8,128)}, u32[]{:S(2)}, u32[]{:S(2)}) collective-permute-start(f32[3,128,128]{2,1,0:T(8,128)S(1)} %get-tuple-element.31), channel_id=1, source_target_pairs={{0,17},{1,18},{2,19},{3,20},{4,21},{5,22},{6,23},{7,24},{8,25},{9,... | collective-permute-start | bytes 589832 | tf_op jit(solution)/shard_map/ppermute | solution.py:23
  182.6 10.4 %collective-permute-start.4 = (f32[3,128,128]{2,1,0:T(8,128)S(1)}, f32[3,128,128]{2,1,0:T(8,128)}, u32[]{:S(2)}, u32[]{:S(2)}) collective-permute-start(f32[3,128,128]{2,1,0:T(8,128)S(1)} %get-tuple-element.32), channel_id=1, source_target_pairs={{0,16},{1,17},{2,18},{3,19},{4,20},{5,21},{6,22},{7,23},{8,24},{9,... | collective-permute-start | bytes 589832 | tf_op jit(solution)/shard_map/ppermute | solution.py:23

commit v2 on v1

v2 whole, which is shorter than its diff:
```python
import functools
import math

import jax
import jax.numpy as jnp
import numpy as np
from jax import lax
from jax.experimental import pallas as pl
from jax.experimental.pallas import tpu as pltpu
from jax.sharding import Mesh
from jax.sharding import PartitionSpec as P

TY = ("ty_0", "ty_1")
PART = ("tx", "ty_0", "ty_1")

high = lax.Precision.HIGHEST
three = lax.Precision.HIGH

IN_VMEM = pl.BlockSpec(memory_space=pltpu.VMEM)
IN_SMEM = pl.BlockSpec(memory_space=pltpu.SMEM)


def moved(value, down, right):
    rows = lax.axis_size("tx")
    cols = lax.axis_size("ty_0") * lax.axis_size("ty_1")
    pairs = [
        (i * cols + j, ((i + down) % rows) * cols + (j + right) % cols)
        for i in range(rows)
        for j in range(cols)
    ]
    return lax.ppermute(value, PART, pairs)


def exchanged(blocks, axis):
    return lax.all_to_all(blocks, axis, split_axis=0, concat_axis=0, tiled=True)


def copied_to_all(block, axis):
    count = lax.axis_size(axis)
    return exchanged(jnp.broadcast_to(block[None], (count, *block.shape)), axis)


def tables(frame):
    grid = np.arange(frame)
    angle = (grid[:, None] * grid[None, :] % frame) * (2.0 * math.pi / frame)
    scale = 1.0 / math.sqrt(frame)
    return np.stack([np.cos(angle) * scale, np.sin(angle) * scale]).astype(np.float32)


def eights(start):
    base = pl.multiple_of((start // 8) * 8, 8)
    return base, start - base


def probe_kernel(wts, counts, eig, probe, note, *, slots, modes):
    frame = eig.shape[2]
    rows = 32
    count = counts[0, 0]
    sums = []
    for s in range(slots):
        sums.append(jnp.zeros((rows, frame), jnp.float32))
    for start in range(0, frame, rows):
        at = pl.ds(start, rows)
        parts = [[jnp.zeros((rows, frame), jnp.float32) for _ in range(slots)] for _ in range(2)]
        for k in range(modes):
            for c in range(2):
                image = eig[c, k, at, :].astype(jnp.float32)
                for s in range(slots):
                    parts[c][s] = parts[c][s] + wts[s, k] * image
        for s in range(slots):
            probe[0, s, at, :] = parts[0][s]
            probe[1, s, at, :] = parts[1][s]
            sums[s] = sums[s] + parts[0][s] * parts[0][s] + parts[1][s] * parts[1][s]
    total = jnp.zeros((rows, frame), jnp.float32)
    for s in range(slots):
        total = total + jnp.where(s < count, sums[s], 0.0)
    illum = jnp.sum(total)
    row = lax.broadcasted_iota(jnp.int32, (8, frame), 0)
    lane = lax.broadcasted_iota(jnp.int32, (8, frame), 1)
    lane = jnp.where(row == 0, lane, -1)
    value = jnp.where(row == 1, illum, 0.0)
    for s in range(slots):
        live = jnp.where(s < count, 1.0, 0.0)
        for k in range(modes):
            value = jnp.where(lane == s * modes + k, live * wts[s, k], value)
    note[...] = value


def frame_kernel(
    offs, counts, table, obj, beside, below, corner, probe, amps, note,
    grads, kept, right, down, across,
    region, acc, win, *, slots, share, n_core,
):
    frame = obj.shape[1]
    wide = 2 * frame
    count = counts[0, 0]
    for c in range(2):
        region[c, :frame, :frame] = obj[c]
        region[c, :frame, frame:] = beside[c]
        region[c, frame:, :frame] = below[c]
        region[c, frame:, frame:] = corner[c]
    acc[...] = jnp.zeros_like(acc)
    for s in range(slots):
        base, rest = eights(offs[s, 0])
        col = offs[s, 1]
        for c in range(2):
            tall = region[c, pl.ds(base, frame + 8), :]
            tall = pltpu.roll(tall, (frame + 8 - rest) % (frame + 8), 0)[:frame]
            win[c, s] = pltpu.roll(tall, (wide - col) % wide, 1)[:, :frame]
    cos = table[0]
    sin = table[1]
    stacked = jnp.concatenate([cos, sin], axis=0)
    side = jnp.concatenate([cos, sin], axis=1)

    def transform(reals, imags, sign):
        both = jnp.concatenate(reals + imags, axis=1)
        left = jnp.dot(stacked, both, precision=three, preferred_element_type=jnp.float32)
        up, low = left[:frame], left[frame:]
        half = slots * frame
        mid = []
        for s in range(slots):
            a = s * frame
            mid.append(up[:, a : a + frame] + sign * low[:, half + a : half + a + frame])
        for s in range(slots):
            a = s * frame
            mid.append(up[:, half + a : half + a + frame] - sign * low[:, a : a + frame])
        tall = jnp.concatenate(mid, axis=0)
        out = jnp.dot(tall, side, precision=three, preferred_element_type=jnp.float32)
        out_re, out_im = [], []
        for s in range(slots):
            a = s * frame
            re, im = out[a : a + frame], out[half + a : half + a + frame]
            out_re.append(re[:, :frame] + sign * im[:, frame:])
            out_im.append(im[:, :frame] - sign * re[:, frame:])
        return out_re, out_im

    psi_re, psi_im = [], []
    for s in range(slots):
        psi_re.append(probe[0, s] * win[0, s] - probe[1, s] * win[1, s])
        psi_im.append(probe[0, s] * win[1, s] + probe[1, s] * win[0, s])
    spec_re, spec_im = transform(psi_re, psi_im, 1.0)
    for s in range(slots):
        live = jnp.where(s < count, 1.0, 0.0)
        power = spec_re[s] * spec_re[s] + spec_im[s] * spec_im[s] + 0.25
        factor = (amps[s].astype(jnp.float32) / jnp.sqrt(power) - 1.0) * live
        spec_re[s] = spec_re[s] * factor
        spec_im[s] = spec_im[s] * factor
    chi_re, chi_im = transform(spec_re, spec_im, -1.0)
    for s in range(slots):
        live = jnp.where(s < count, 1.0, 0.0)
        image = (
            win[0, s] * chi_re[s] + win[1, s] * chi_im[s],
            win[0, s] * chi_im[s] - win[1, s] * chi_re[s],
        )
        for d in range(grads.shape[0]):
            a = (d // n_core) * share
            grads[d, s * share : (s + 1) * share, :] = image[d % n_core][a : a + share]
        pieces = (
            probe[0, s] * chi_re[s] + probe[1, s] * chi_im[s],
            probe[0, s] * chi_im[s] - probe[1, s] * chi_re[s],
            (probe[0, s] * probe[0, s] + probe[1, s] * probe[1, s]) * live,
        )
        base, rest = eights(offs[s, 0])
        col = offs[s, 1]
        at = pl.ds(base, frame + 8)
        for q in range(3):
            spread = jnp.concatenate([pieces[q], jnp.zeros_like(pieces[q])], axis=1)
            spread = pltpu.roll(spread, col, 1)
            spread = jnp.concatenate([spread, jnp.zeros((8, wide), jnp.float32)], axis=0)
            acc[q, at, :] = acc[q, at, :] + pltpu.roll(spread, rest, 0)
    for d in range(grads.shape[0]):
        grads[d, slots * share :, :] = note[...]
    for q in range(3):
        kept[q] = acc[q, :frame, :frame]
        right[q] = acc[q, :frame, frame:]
        down[q] = acc[q, frame:, :frame]
        across[q] = acc[q, frame:, frame:]


def mode_kernel(row, sent, *, slots, modes, share):
    sources, depth, frame = row.shape
    notes = jnp.concatenate([row[d, slots * share : slots * share + 1, :] for d in range(sources)], axis=0)
    wts = jnp.concatenate([notes[:, s * modes : (s + 1) * modes] for s in range(slots)], axis=0)
    columns = []
    for r in range(share):
        columns.append(
            jnp.concatenate(
                [
                    jnp.concatenate([row[d, s * share + r : s * share + r + 1, :] for d in range(sources)], axis=0)
                    for s in range(slots)
                ],
                axis=0,
            )
        )
    dims = (((0,), (0,)), ((), ()))
    images = lax.dot_general(
        wts, jnp.concatenate(columns, axis=1), dims, precision=high, preferred_element_type=jnp.float32
    )
    norms = lax.dot_general(
        wts * wts, jnp.ones((slots * sources, frame), jnp.float32), dims,
        precision=high, preferred_element_type=jnp.float32,
    )
    illum = jnp.zeros((1, frame), jnp.float32)
    for d in range(sources):
        illum = illum + row[d, slots * share + 1 : slots * share + 2, :]
    for r in range(share):
        sent[:, r, :] = images[:, r * frame : (r + 1) * frame]
    sent[:, share, :] = norms
    for r in range(share + 1, share + 8):
        sent[:, r, :] = jnp.broadcast_to(illum, (modes, frame))


def update_kernel(parts, own, copies, illum, *, share):
    total = parts[0]
    for d in range(1, parts.shape[0]):
        total = total + parts[d]
    fresh = own[...].astype(jnp.float32) + total[:share] / (total[share : share + 1] + 1.0)
    for d in range(copies.shape[0]):
        copies[d] = fresh
    illum[...] = total[share:]


def per_device(obj_field, eigenprobes, weights, offsets, counts, amplitudes):
    tile = obj_field.shape[1]
    modes = eigenprobes.shape[1]
    frame = eigenprobes.shape[2]
    slots = weights.shape[2]
    n_tx = lax.axis_size("tx")
    n_chip = lax.axis_size("ty_0")
    n_core = lax.axis_size("ty_1")
    n_ty = n_chip * n_core
    share = frame // n_chip
    f32 = jnp.float32
    wts = weights[0, 0]
    offs = offsets[0, 0]
    below = moved(obj_field, -1, 0)
    beside = moved(obj_field, 0, -1)
    corner = moved(obj_field, -1, -1)
    probe, note = pl.pallas_call(
        functools.partial(probe_kernel, slots=slots, modes=modes),
        out_shape=(
            jax.ShapeDtypeStruct((2, slots, frame, frame), f32),
            jax.ShapeDtypeStruct((8, frame), f32),
        ),
        in_specs=[IN_SMEM, IN_SMEM, IN_VMEM],
        out_specs=(IN_VMEM, IN_VMEM),
    )(wts, counts, eigenprobes)
    core = lax.axis_index("ty_1")
    own = lax.dynamic_slice(
        eigenprobes,
        (core, lax.axis_index("tx"), lax.axis_index("ty_0") * share, jnp.int32(0)),
        (1, 1, share, frame),
    )[0, 0]
    quadrant = jax.ShapeDtypeStruct((3, tile, tile), f32)
    grads, kept, right, down, across = pl.pallas_call(
        functools.partial(frame_kernel, slots=slots, share=share, n_core=n_core),
        out_shape=(
            jax.ShapeDtypeStruct((n_ty, slots * share + 8, frame), f32),
            quadrant, quadrant, quadrant, quadrant,
        ),
        in_specs=[IN_SMEM, IN_SMEM] + [IN_VMEM] * 8,
        out_specs=(IN_VMEM,) * 5,
        scratch_shapes=[
            pltpu.VMEM((2, 2 * frame, 2 * frame), f32),
            pltpu.VMEM((3, 2 * frame, 2 * frame), f32),
            pltpu.VMEM((2, slots, frame, frame), f32),
        ],
    )(offs, counts, tables(frame), obj_field, beside, below, corner, probe, amplitudes[0, 0], note)
    row = exchanged(grads, TY)
    from_left = moved(right, 0, 1)
    from_above = moved(down, 1, 0)
    from_corner = moved(across, 1, 1)
    sent = pl.pallas_call(
        functools.partial(mode_kernel, slots=slots, modes=modes, share=share),
        out_shape=jax.ShapeDtypeStruct((modes, share + 8, frame), f32),
        in_specs=[IN_VMEM],
        out_specs=IN_VMEM,
    )(row)
    parts = exchanged(sent, "tx")
    copies, illum = pl.pallas_call(
        functools.partial(update_kernel, share=share),
        out_shape=(
            jax.ShapeDtypeStruct((n_tx, share, frame), f32),
            jax.ShapeDtypeStruct((8, frame), f32),
        ),
        in_specs=[IN_VMEM, IN_VMEM],
        out_specs=(IN_VMEM, IN_VMEM),
    )(parts, own)
    column = exchanged(copies, "tx")
    half = copied_to_all(column, "ty_0").reshape(n_chip, modes, share, frame)
    other = lax.ppermute(half, "ty_1", [(0, 1), (1, 0)])
    half = half.transpose(1, 0, 2, 3).reshape(modes, frame, frame)
    other = other.transpose(1, 0, 2, 3).reshape(modes, frame, frame)
    first = core == 0
    new_eig = jnp.stack([jnp.where(first, half, other), jnp.where(first, other, half)])

    totals = kept + from_left + from_above + from_corner
    cells = n_tx * n_ty * tile * tile
    mean_illum = illum[1, 0] / cells
    new_object = obj_field + totals[:2] / (totals[2] + mean_illum)[None]
    return (new_object, new_eig)


def solution(mesh):
    finer = Mesh(
        mesh.devices.reshape(mesh.shape["grp"], mesh.shape["tx"], -1, 2),
        ("grp", "tx", "ty_0", "ty_1"),
    )
    return jax.shard_map(
        per_device,
        mesh=finer,
        in_specs=(
            P(None, ("grp", "tx"), TY),
            P(None, "grp", None, None),
            P(("grp", "tx"), TY, None, None),
            P(("grp", "tx"), TY, None, None),
            P(("grp", "tx"), TY),
            P(("grp", "tx"), TY, None, None, None),
        ),
        out_specs=(P(None, ("grp", "tx"), TY), P(None, "grp", None, None)),
        check_vma=False,
    )
```

time: 199 us -> 182 us (0.915)
  blocking collectives: 41.3 us -> 70.9 us
  waiting for transfers between devices: 39.6 us -> 23.6 us
  matrix products: 14.2 us -> 0 us
  Pallas kernels: 0 us -> 11.9 us
  between operations: 13.5 us -> 2.09 us
  local copies, waits for them, and re-layouts: 16.3 us -> 6.65 us
  starting transfers between devices: 66.5 us -> 62.9 us
  other arithmetic: 6.26 us -> 3.51 us
    all_to_all x2 -> x3, blocking collectives: 41.3 us -> 70.9 us  [exchanged(): return lax.all_to_all(blocks, axis, split_axis=0, concat_axis=0, tiled=True)]
    all_to_all x2 -> x1, waiting for transfers between devices: 31.4 us -> 12.9 us  [exchanged(): return lax.all_to_all(blocks, axis, split_axis=0, concat_axis=0, tiled=True)]
    dot_general x18 -> x0, matrix products: 14.2 us -> none  [the longest x1 2.21 us: per_device(): probe = jnp.einsum('sk,ckij->csij', wts, eig32, precision=high)]
    pallas_call x0 -> x4, Pallas kernels: none -> 11.9 us  [the longest x1 5.55 us: per_device(): pl.pallas_call(functools.partial(frame_kernel, slots=slots, share=share,...]
    dynamic_update_slice x3 -> x0, local copies, waits for them, and re-layouts: 8.48 us -> none  [per_device(): acc = lax.dynamic_update_slice(acc, current + pieces[s], at)]
    all_to_all x2 -> x1, starting transfers between devices: 7.73 us -> 3.96 us  [exchanged(): return lax.all_to_all(blocks, axis, split_axis=0, concat_axis=0, tiled=True)]
    unnamed x4 -> x13, local copies, waits for them, and re-layouts: 0.01 us -> 2.65 us
    squeeze x2, local copies, waits for them, and re-layouts: 0.1 us -> 2.62 us  [the longest x1 1.33 us: per_device(): offs = offsets[0, 0]]
  transfers between devices with their start and end apart: 9 -> 8, of which waited for: 4 -> 3; matrix products, arithmetic and copies ran while one was open for 8% -> 4% of each run, Pallas kernels for 0% -> 1%
where the time goes in v2:
time: 182 us; the launch traced here: 181 us
  blocking collectives  70.9 us (39%)
  starting transfers between devices  62.9 us (35%)
  waiting for transfers between devices  23.6 us (13%)
  Pallas kernels  11.9 us (7%)
  local copies, waits for them, and re-layouts  6.65 us (4%)
  other arithmetic  3.51 us (2%)
  between operations  2.09 us (1%)
    all_to_all x3, blocking collectives, exchanged(): return lax.all_to_all(blocks, axis, split_axis=0, concat_axis=0, tiled=True)  70.9 us
    ppermute x6, starting transfers between devices, moved(): return lax.ppermute(value, PART, pairs)  57 us
    all_to_all x1, waiting for transfers between devices, exchanged(): return lax.all_to_all(blocks, axis, split_axis=0, concat_axis=0, tiled=True)  12.9 us
    ppermute x6, waiting for transfers between devices, moved(): return lax.ppermute(value, PART, pairs)  10.7 us
    pallas_call x1, Pallas kernels, per_device(): pl.pallas_call(functools.partial(frame_kernel, slots=slots, share=share,...  5.55 us
    all_to_all x1, starting transfers between devices, exchanged(): return lax.all_to_all(blocks, axis, split_axis=0, concat_axis=0, tiled=True)  3.96 us
  transfers between devices with their start and end apart: 8, of which 3 were waited for; matrix products, arithmetic and copies ran while one was open for 4% of the time, Pallas kernels for 1%

profile of v2, /device:TPU:80, one launch (start us, length us, event | category | flops | bytes accessed | tf_op | source)
XLA Modules:
  0.0 181.5 jit_solution(6180571733964223016)
XLA Ops:
  0.6 46.8 %collective-permute-start.2 = (f32[2,128,128]{2,1,0:T(8,128)}, f32[2,128,128]{2,1,0:T(8,128)S(1)}, u32[]{:S(2)}, u32[]{:S(2)}) collective-permute-start(f32[2,128,128]{2,1,0:T(8,128)} %obj.1), channel_id=1, source_target_pairs={{0,255},{1,240},{2,241},{3,242},{4,243},{5,244},{6,245},{7,246},{8... | collective-permute-start | bytes 393224 | tf_op jit(solution)/shard_map/ppermute | solution.py:31
  47.4 2.0 %collective-permute-start.1 = (f32[2,128,128]{2,1,0:T(8,128)}, f32[2,128,128]{2,1,0:T(8,128)S(1)}, u32[]{:S(2)}, u32[]{:S(2)}) collective-permute-start(f32[2,128,128]{2,1,0:T(8,128)} %obj.1), channel_id=1, source_target_pairs={{0,240},{1,241},{2,242},{3,243},{4,244},{5,245},{6,246},{7,247},{8... | collective-permute-start | bytes 393224 | tf_op jit(solution)/shard_map/ppermute | solution.py:31
  49.4 0.8 collective-permute-start
  50.9 1.3 copy.19
  52.1 1.3 copy.11.offs
  53.5 2.5 %shard_map.86 = (f32[2,3,128,128]{3,2,1,0:T(8,128)}, f32[8,128]{1,0:T(8,128)}) custom-call(f32[3,16]{1,0:T(4,128)} %bitcast.19, s32[1,1]{1,0:T(1,128)S(6)} %copy.20.counts, bf16[2,16,128,128]{3,2,1,0:T(8,128)(2,1)} %eig.1), custom_call_target="tpu_custom_call" | custom-call | tf_op jit(solution)/shard_map/pallas_call | solution.py:239
  56.7 5.5 %shard_map.87 = (f32[16,56,128]{2,1,0:T(8,128)}, f32[3,128,128]{2,1,0:T(8,128)}, f32[3,128,128]{2,1,0:T(8,128)}, f32[3,128,128]{2,1,0:T(8,128)}, f32[3,128,128]{2,1,0:T(8,128)}) custom-call(s32[3,2]{1,0:T(4,128)} %copy.11.offs, s32[1,1]{1,0:T(1,128)S(6)} %copy.20.counts, f32[2,128,128]{2,1,0:T(8,128)} %constant.27.clone.table, f32[2,128,128]{2,1,0:T(8,128)} %obj.1, ...), custom_call_target="tpu_custom_call" | custom-call | tf_op jit(solution)/shard_map/pallas_call | solution.py:255
  62.3 19.1 %all_to_all.20.row = f32[16,56,128]{2,1,0:T(8,128)} all-to-all(f32[16,56,128]{2,1,0:T(8,128)} %get-tuple-element.17), channel_id=1, replica_groups=mesh['grp'=2,'tx'=16,'ty_0'=8,'ty_1'=2] {'ty_0','ty_1'}, dimensions={0} | all-to-all | bytes 917504 | tf_op jit(solution)/shard_map/all_to_all | solution.py:35
  81.4 2.2 %shard_map.88 = f32[16,24,128]{2,1,0:T(8,128)} custom-call(f32[16,56,128]{2,1,0:T(8,128)} %all_to_all.20.row), custom_call_target="tpu_custom_call" | custom-call | tf_op jit(solution)/shard_map/pallas_call | solution.py:273
  83.6 4.0 %all-to-all-start.1 = ((f32[16,24,128]{2,1,0:T(8,128)}), f32[16,24,128]{2,1,0:T(8,128)S(1)}, u32[]{:S(2)}, u32[]{:S(2)}) async-start(f32[16,24,128]{2,1,0:T(8,128)} %shard_map.88), calls=%async_computation.1 | async-start | bytes 393216 | tf_op jit(solution)/shard_map/all_to_all | solution.py:35
  87.5 1.3 dynamic-slice_bitcast_fusion.own
  88.8 12.9 %all-to-all-done.1.parts = f32[16,24,128]{2,1,0:T(8,128)S(1)} async-done(((f32[16,24,128]{2,1,0:T(8,128)}), f32[16,24,128]{2,1,0:T(8,128)S(1)}, u32[]{:S(2)}, u32[]{:S(2)}) %all-to-all-start.1) | async-done | bytes 196640 | tf_op jit(solution)/shard_map/all_to_all | solution.py:35
  102.4 1.6 shard_map.89
  104.0 22.7 %all_to_all.21 = f32[16,16,128]{2,1,0:T(8,128)S(1)} all-to-all(f32[16,16,128]{2,1,0:T(8,128)} %get-tuple-element.19), channel_id=1, replica_groups=mesh['grp'=2,'tx'=16,'ty_0'=8,'ty_1'=2] {'tx'}, dimensions={0} | all-to-all | bytes 262144 | tf_op jit(solution)/shard_map/all_to_all | solution.py:35
  126.8 29.0 %all_to_all.22 = f32[8,16,16,128]{3,2,1,0:T(8,128)S(1)} all-to-all(f32[8,16,16,128]{3,2,1,0:T(8,128)S(1)} %broadcast_in_dim.2), channel_id=1, replica_groups=mesh['grp'=2,'tx'=16,'ty_0'=8,'ty_1'=2] {'ty_0'}, dimensions={0} | all-to-all | bytes 2097152 | tf_op jit(solution)/shard_map/all_to_all | solution.py:35
  156.0 2.0 %collective-permute-start.6 = (f32[8,16,16,128]{3,2,0,1:T(8,128)S(1)}, f32[8,16,16,128]{3,2,0,1:T(8,128)S(1)}, u32[]{:S(2)}, u32[]{:S(2)}) collective-permute-start(f32[8,16,16,128]{3,2,0,1:T(8,128)S(1)} %copy.13), channel_id=1, source_target_pairs={{0,1},{1,0},{2,3},{3,2},{4,5},{5,4},{6,7},{7,6},{8,9},{9,8},{10,11... | collective-permute-start | bytes 3145736 | tf_op jit(solution)/shard_map/ppermute | solution.py:291
  158.5 4.9 %collective-permute-start.4 = (f32[3,128,128]{2,1,0:T(8,128)}, f32[3,128,128]{2,1,0:T(8,128)}, u32[]{:S(2)}, u32[]{:S(2)}) collective-permute-start(f32[3,128,128]{2,1,0:T(8,128)} %get-tuple-element.15), channel_id=1, source_target_pairs={{0,16},{1,17},{2,18},{3,19},{4,20},{5,21},{6,22},{7,23},{8,24},{9,... | collective-permute-start | bytes 589832 | tf_op jit(solution)/shard_map/ppermute | solution.py:31
  163.4 2.0 %collective-permute-start.5 = (f32[3,128,128]{2,1,0:T(8,128)}, f32[3,128,128]{2,1,0:T(8,128)}, u32[]{:S(2)}, u32[]{:S(2)}) collective-permute-start(f32[3,128,128]{2,1,0:T(8,128)} %get-tuple-element.16), channel_id=1, source_target_pairs={{0,17},{1,18},{2,19},{3,20},{4,21},{5,22},{6,23},{7,24},{8,25},{9,... | collective-permute-start | bytes 589832 | tf_op jit(solution)/shard_map/ppermute | solution.py:31
  165.4 3.7 %collective-permute-done.4 = f32[3,128,128]{2,1,0:T(8,128)} collective-permute-done((f32[3,128,128]{2,1,0:T(8,128)}, f32[3,128,128]{2,1,0:T(8,128)}, u32[]{:S(2)}, u32[]{:S(2)}) %collective-permute-start.4) | collective-permute-done | bytes 196640 | tf_op jit(solution)/shard_map/ppermute | solution.py:31
  169.1 7.0 %collective-permute-done.5 = f32[3,128,128]{2,1,0:T(8,128)} collective-permute-done((f32[3,128,128]{2,1,0:T(8,128)}, f32[3,128,128]{2,1,0:T(8,128)}, u32[]{:S(2)}, u32[]{:S(2)}) %collective-permute-start.5) | collective-permute-done | bytes 196640 | tf_op jit(solution)/shard_map/ppermute | solution.py:31
  176.1 1.2 add_add_fusion
  177.2 1.2 slice.11
  179.1 0.7 fusion
  180.0 1.5 pad_maximum_fusion
  (22 shorter events, 2.3 us)
Async XLA Ops:
  0.6 55.3 %collective-permute-start.2 = (f32[2,128,128]{2,1,0:T(8,128)}, f32[2,128,128]{2,1,0:T(8,128)S(1)}, u32[]{:S(2)}, u32[]{:S(2)}) collective-permute-start(f32[2,128,128]{2,1,0:T(8,128)} %obj.1), channel_id=1, source_target_pairs={{0,255},{1,240},{2,241},{3,242},{4,243},{5,244},{6,245},{7,246},{8... | collective-permute-start | bytes 393224 | tf_op jit(solution)/shard_map/ppermute | solution.py:31
  47.4 8.5 %collective-permute-start.1 = (f32[2,128,128]{2,1,0:T(8,128)}, f32[2,128,128]{2,1,0:T(8,128)S(1)}, u32[]{:S(2)}, u32[]{:S(2)}) collective-permute-start(f32[2,128,128]{2,1,0:T(8,128)} %obj.1), channel_id=1, source_target_pairs={{0,240},{1,241},{2,242},{3,243},{4,244},{5,245},{6,246},{7,247},{8... | collective-permute-start | bytes 393224 | tf_op jit(solution)/shard_map/ppermute | solution.py:31
  49.4 6.6 %collective-permute-start = (f32[2,128,128]{2,1,0:T(8,128)}, f32[2,128,128]{2,1,0:T(8,128)S(1)}, u32[]{:S(2)}, u32[]{:S(2)}) collective-permute-start(f32[2,128,128]{2,1,0:T(8,128)} %obj.1), channel_id=1, source_target_pairs={{0,15},{1,0},{2,1},{3,2},{4,3},{5,4},{6,5},{7,6},{8,7},{9,8},{10,9... | collective-permute-start | bytes 393224 | tf_op jit(solution)/shard_map/ppermute | solution.py:31
  56.0 0.7 copy-start.3
  56.0 0.7 copy-start.4
  56.0 0.7 copy-start.5
  83.6 18.1 %all-to-all-start.1 = ((f32[16,24,128]{2,1,0:T(8,128)}), f32[16,24,128]{2,1,0:T(8,128)S(1)}, u32[]{:S(2)}, u32[]{:S(2)}) async-start(f32[16,24,128]{2,1,0:T(8,128)} %shard_map.88), calls=%async_computation.1 | async-start | bytes 393216 | tf_op jit(solution)/shard_map/all_to_all | solution.py:35
  101.7 0.7 copy-start
  126.8 49.3 %copy-start.2 = (f32[3,128,128]{2,1,0:T(8,128)S(1)}, f32[3,128,128]{2,1,0:T(8,128)}, u32[]{:S(2)}) copy-start(f32[3,128,128]{2,1,0:T(8,128)} %get-tuple-element.13) | copy-start | bytes 589828
  155.9 23.3 %copy-start.1 = (f32[2,128,128]{2,1,0:T(8,128)S(1)}, f32[2,128,128]{2,1,0:T(8,128)}, u32[]{:S(2)}) copy-start(f32[2,128,128]{2,1,0:T(8,128)} %obj.1) | copy-start | bytes 393220
  156.0 23.8 %collective-permute-start.6 = (f32[8,16,16,128]{3,2,0,1:T(8,128)S(1)}, f32[8,16,16,128]{3,2,0,1:T(8,128)S(1)}, u32[]{:S(2)}, u32[]{:S(2)}) collective-permute-start(f32[8,16,16,128]{3,2,0,1:T(8,128)S(1)} %copy.13), channel_id=1, source_target_pairs={{0,1},{1,0},{2,3},{3,2},{4,5},{5,4},{6,7},{7,6},{8,9},{9,8},{10,11... | collective-permute-start | bytes 3145736 | tf_op jit(solution)/shard_map/ppermute | solution.py:291
  157.9 7.4 %collective-permute-start.3 = (f32[3,128,128]{2,1,0:T(8,128)}, f32[3,128,128]{2,1,0:T(8,128)}, u32[]{:S(2)}, u32[]{:S(2)}) collective-permute-start(f32[3,128,128]{2,1,0:T(8,128)} %get-tuple-element.14), channel_id=1, source_target_pairs={{0,1},{1,2},{2,3},{3,4},{4,5},{5,6},{6,7},{7,8},{8,9},{9,10},{10,1... | collective-permute-start | bytes 589832 | tf_op jit(solution)/shard_map/ppermute | solution.py:31
  158.5 10.6 %collective-permute-start.4 = (f32[3,128,128]{2,1,0:T(8,128)}, f32[3,128,128]{2,1,0:T(8,128)}, u32[]{:S(2)}, u32[]{:S(2)}) collective-permute-start(f32[3,128,128]{2,1,0:T(8,128)} %get-tuple-element.15), channel_id=1, source_target_pairs={{0,16},{1,17},{2,18},{3,19},{4,20},{5,21},{6,22},{7,23},{8,24},{9,... | collective-permute-start | bytes 589832 | tf_op jit(solution)/shard_map/ppermute | solution.py:31
  163.4 12.7 %collective-permute-start.5 = (f32[3,128,128]{2,1,0:T(8,128)}, f32[3,128,128]{2,1,0:T(8,128)}, u32[]{:S(2)}, u32[]{:S(2)}) collective-permute-start(f32[3,128,128]{2,1,0:T(8,128)} %get-tuple-element.16), channel_id=1, source_target_pairs={{0,17},{1,18},{2,19},{3,20},{4,21},{5,22},{6,23},{7,24},{8,25},{9,... | collective-permute-start | bytes 589832 | tf_op jit(solution)/shard_map/ppermute | solution.py:31
